TPU v7x, 128 devices: a whole 4x4x4 slice. The times are simulated.
128 devices in a mesh: row: 8 (over x, core), col: 16 (over y, z).
Axes of the slice: x: 4, y: 4, z: 4, core: 2. Of those that a mesh axis runs over, the one named last changes fastest.
Arguments:
- panel_rows: float32 [8192, 4096], P('row', 'col'), may hold values from -0.75 to 0.75
- owner_slot: int32 [16, 16], replicated, may hold values from -1 to 31, as said below
Outputs:
- packed: float32 [8, 32, 512, 512], P('row', 'col')
Inputs may be any that keep to these rules, and one draw needn't show every extreme that they name: For j <= i, owner_slot[i, j] is the position of tile (i, j) among the 32 positions of group i // 2; tiles of one group have distinct positions; entries above the diagonal are -1. Position p lies on the device of col index p // 2.
All inputs are finite; a program needn't handle non-finite values.
Results may differ from a plain program's by a relative error of at most 0.0003.
Values sent between devices are 32-bit elements; how exact they have to be, the bound alone decides.
No kernel may reach another device: no remote copies, remote signals or barrier semaphores. Data moves between devices by JAX's collectives and lax.ppermute only.
A program may use at most 128 MiB of HBM per device.

v0:
```python
import jax
import jax.numpy as jnp
from jax import lax
from jax.sharding import PartitionSpec as P

BLOCK = 512


def slot_table(owner_slot, group_id, positions, per_group):
    blocks = owner_slot.shape[0]
    block_row = jnp.arange(blocks, dtype=jnp.int32)[:, None]
    block_col = jnp.arange(blocks, dtype=jnp.int32)[None, :]
    inside = (block_row // per_group == group_id) & (block_col <= block_row)
    wanted = jnp.arange(positions, dtype=jnp.int32)[:, None, None]
    matched = inside[None] & (owner_slot[None] == wanted)
    is_live = jnp.any(matched, axis=(1, 2))
    left_block = jnp.sum(jnp.where(matched, block_row[None], 0), axis=(1, 2))
    right_block = jnp.sum(jnp.where(matched, block_col[None], 0), axis=(1, 2))
    return (left_block, right_block, is_live)


def tile_products(tiles_all, lefts, rights, flags):

    def single(packed_item):
        left_one, right_one, flag = packed_item

        def compute():
            return lax.dot_general(
                tiles_all[left_one],
                tiles_all[right_one],
                (((1,), (1,)), ((), ())),
                precision=lax.Precision.HIGHEST,
                preferred_element_type=jnp.float32,
            )

        def blank():
            return jnp.zeros((BLOCK, BLOCK), jnp.float32)

        return lax.cond(flag, compute, blank)

    return lax.map(single, (lefts, rights, flags))


def body(panel_rows, owner_slot):
    rows_n = lax.axis_size("row")
    cols_n = lax.axis_size("col")
    slab_rows, inner_cols = panel_rows.shape
    per_group = slab_rows // BLOCK
    blocks = per_group * rows_n
    row_tiles = per_group * (blocks - per_group) + per_group * (per_group + 1) // 2
    slot_count = (row_tiles + cols_n - 1) // cols_n
    positions = cols_n * slot_count
    gathered = lax.all_gather(panel_rows, "row", axis=0, tiled=True)
    my_group = lax.axis_index("row")
    left_block, right_block, is_live = slot_table(owner_slot, my_group, positions, per_group)
    tiles_all = gathered.reshape(blocks, BLOCK, inner_cols)
    summed = lax.psum_scatter(
        tile_products(tiles_all, left_block, right_block, is_live),
        "col",
        scatter_dimension=0,
        tiled=True,
    )
    return summed[None]


def solution(mesh):
    placed = (P("row", "col"), P())
    return jax.shard_map(
        body, mesh=mesh, in_specs=placed, out_specs=P("row", "col", None, None), check_vma=False
    )
```

profile of v0, /device:TPU:1, one launch (start us, length us, event | category | flops | bytes accessed | tf_op | source)
XLA Modules:
  0.0 575.0 jit_solution(2577626217838474993)
XLA Ops:
  6.5 0.7 all-gather.2.cloned.1.call-update
  7.4 0.8 fusion.6
  8.3 0.8 select_reduce_fusion
  9.1 53.2 %all-gather.2.cloned.1.call-done = f32[8192,256]{1,0:T(8,128)} async-done(((f32[1024,256]{1,0:T(8,128)}), f32[8192,256]{1,0:T(8,128)}) %all-gather.2.cloned.1.call-update) | async-done | bytes 8388624 | tf_op jit(solution)/shard_map/all_gather | solution.py:53
  62.3 133.3 %while.10 = (s32[]{:T(128)}, f32[32,512,512]{2,1,0:T(8,128)}, pred[32]{0:T(512)(128)(4,1)S(1)}, s32[32]{0:T(128)S(1)}, f32[16,512,256]{2,1,0:T(8,128)}, /*index=5*/s32[32]{0:T(128)S(1)}, s32[]{:T(128)}) while((s32[]{:T(128)}, f32[32,512,512]{2,1,0:T(8,128)}, pred[32]{0:T(512)(128)(4,1)S(1)}, s32[32]{0:T(128)S(1)}, f32[16,512,256]{2,1,0:T(8,128)}, ...), condition=%wide.region_6.7_spmd, body=%wide.region_3.6_spmd.sunk | while | flops 805306368 | bytes 4195044 | solution.py:41
  63.6 7.6 %conditional.2 = (f32[1,512,512]{2,1,0:T(8,128)S(1)}) conditional(s32[]{:T(128)} %bitcast.14, () %tuple.31, (s32[32]{0:T(128)S(1)}, s32[]{:T(128)}, f32[16,512,256]{2,1,0:T(8,128)}, s32[32]{0:T(128)S(1)}) %tuple.32), branch_computations={%region_4.4_spmd, %region_5.5_spmd} | conditional | flops 805306368 | bytes 2097260 | solution.py:39
  63.6 0.7 dynamic_slice.18
  66.3 0.7 dynamic_slice.20
  69.0 2.2 convolution_bitcast_fusion
  71.2 1.1 constant_dynamic-update-slice_fusion.2
  73.7 1.1 constant_dynamic-update-slice_fusion.2
  76.3 1.1 constant_dynamic-update-slice_fusion.2
  78.8 1.1 constant_dynamic-update-slice_fusion.2
  81.4 1.0 constant_dynamic-update-slice_fusion.2
  83.9 1.1 constant_dynamic-update-slice_fusion.2
  86.3 7.6 %conditional.2 = (f32[1,512,512]{2,1,0:T(8,128)S(1)}) conditional(s32[]{:T(128)} %bitcast.14, () %tuple.31, (s32[32]{0:T(128)S(1)}, s32[]{:T(128)}, f32[16,512,256]{2,1,0:T(8,128)}, s32[32]{0:T(128)S(1)}) %tuple.32), branch_computations={%region_4.4_spmd, %region_5.5_spmd} | conditional | flops 805306368 | bytes 2097260 | solution.py:39
  86.3 0.7 dynamic_slice.18
  89.0 0.7 dynamic_slice.20
  91.6 2.2 convolution_bitcast_fusion
  93.9 1.1 constant_dynamic-update-slice_fusion.2
  96.4 1.0 constant_dynamic-update-slice_fusion.2
  98.8 7.6 %conditional.2 = (f32[1,512,512]{2,1,0:T(8,128)S(1)}) conditional(s32[]{:T(128)} %bitcast.14, () %tuple.31, (s32[32]{0:T(128)S(1)}, s32[]{:T(128)}, f32[16,512,256]{2,1,0:T(8,128)}, s32[32]{0:T(128)S(1)}) %tuple.32), branch_computations={%region_4.4_spmd, %region_5.5_spmd} | conditional | flops 805306368 | bytes 2097260 | solution.py:39
  98.8 0.7 dynamic_slice.18
  101.5 0.7 dynamic_slice.20
  104.1 2.2 convolution_bitcast_fusion
  106.4 1.1 constant_dynamic-update-slice_fusion.2
  109.0 1.0 constant_dynamic-update-slice_fusion.2
  111.5 1.1 constant_dynamic-update-slice_fusion.2
  114.0 1.0 constant_dynamic-update-slice_fusion.2
  116.5 1.1 constant_dynamic-update-slice_fusion.2
  119.1 1.0 constant_dynamic-update-slice_fusion.2
  121.6 1.1 constant_dynamic-update-slice_fusion.2
  124.1 1.1 constant_dynamic-update-slice_fusion.2
  126.7 1.1 constant_dynamic-update-slice_fusion.2
  129.2 1.1 constant_dynamic-update-slice_fusion.2
  131.8 1.1 constant_dynamic-update-slice_fusion.2
  134.3 1.1 constant_dynamic-update-slice_fusion.2
  136.7 7.6 %conditional.2 = (f32[1,512,512]{2,1,0:T(8,128)S(1)}) conditional(s32[]{:T(128)} %bitcast.14, () %tuple.31, (s32[32]{0:T(128)S(1)}, s32[]{:T(128)}, f32[16,512,256]{2,1,0:T(8,128)}, s32[32]{0:T(128)S(1)}) %tuple.32), branch_computations={%region_4.4_spmd, %region_5.5_spmd} | conditional | flops 805306368 | bytes 2097260 | solution.py:39
  136.7 0.7 dynamic_slice.18
  139.4 0.7 dynamic_slice.20
  142.0 2.2 convolution_bitcast_fusion
  144.3 1.1 constant_dynamic-update-slice_fusion.2
  146.6 7.6 %conditional.2 = (f32[1,512,512]{2,1,0:T(8,128)S(1)}) conditional(s32[]{:T(128)} %bitcast.14, () %tuple.31, (s32[32]{0:T(128)S(1)}, s32[]{:T(128)}, f32[16,512,256]{2,1,0:T(8,128)}, s32[32]{0:T(128)S(1)}) %tuple.32), branch_computations={%region_4.4_spmd, %region_5.5_spmd} | conditional | flops 805306368 | bytes 2097260 | solution.py:39
  146.7 0.7 dynamic_slice.18
  149.3 0.7 dynamic_slice.20
  152.0 2.2 convolution_bitcast_fusion
  154.2 1.1 constant_dynamic-update-slice_fusion.2
  156.8 1.1 constant_dynamic-update-slice_fusion.2
  159.2 7.6 %conditional.2 = (f32[1,512,512]{2,1,0:T(8,128)S(1)}) conditional(s32[]{:T(128)} %bitcast.14, () %tuple.31, (s32[32]{0:T(128)S(1)}, s32[]{:T(128)}, f32[16,512,256]{2,1,0:T(8,128)}, s32[32]{0:T(128)S(1)}) %tuple.32), branch_computations={%region_4.4_spmd, %region_5.5_spmd} | conditional | flops 805306368 | bytes 2097260 | solution.py:39
  159.2 0.7 dynamic_slice.18
  161.9 0.7 dynamic_slice.20
  164.5 2.2 convolution_bitcast_fusion
  166.8 1.1 constant_dynamic-update-slice_fusion.2
  169.3 1.1 constant_dynamic-update-slice_fusion.2
  171.9 1.0 constant_dynamic-update-slice_fusion.2
  174.4 1.0 constant_dynamic-update-slice_fusion.2
  176.9 1.0 constant_dynamic-update-slice_fusion.2
  179.4 1.1 constant_dynamic-update-slice_fusion.2
  182.0 1.0 constant_dynamic-update-slice_fusion.2
  184.5 1.1 constant_dynamic-update-slice_fusion.2
  186.9 7.6 %conditional.2 = (f32[1,512,512]{2,1,0:T(8,128)S(1)}) conditional(s32[]{:T(128)} %bitcast.14, () %tuple.31, (s32[32]{0:T(128)S(1)}, s32[]{:T(128)}, f32[16,512,256]{2,1,0:T(8,128)}, s32[32]{0:T(128)S(1)}) %tuple.32), branch_computations={%region_4.4_spmd, %region_5.5_spmd} | conditional | flops 805306368 | bytes 2097260 | solution.py:39
  192.2 2.2 convolution_bitcast_fusion
  194.5 1.1 constant_dynamic-update-slice_fusion.2
  195.6 372.5 %reduce-scatter.2.cloned.1.call-done = f32[2,512,512]{2,1,0:T(8,128)} async-done(((f32[32,512,512]{2,1,0:T(8,128)}), f32[2,512,512]{2,1,0:T(8,128)}) %reduce-scatter.2.cloned.1.call-update) | async-done | bytes 2097168 | tf_op jit(solution)/shard_map/reduce_scatter | solution.py:57
  (90 shorter events, 28.4 us)
Async XLA Ops:
  6.5 55.8 %all-gather.2.cloned.1.call-start = ((), (), s32[]{:S(2)}) async-start(), calls=%async_computation.1 | async-start | bytes 9437184 | tf_op jit(solution)/shard_map/all_gather | solution.py:53
  7.3 560.9 %reduce-scatter.2.cloned.1.call-start = ((), (), s32[]{:S(2)}) async-start(), calls=%async_computation.2 | async-start | bytes 35651584 | tf_op jit(solution)/shard_map/reduce_scatter | solution.py:57
Sparse Core Ops, SparseCore 0:
  9.0 53.2 all-gather.1
  195.7 372.3 reduce-scatter.1
where the time goes:
time: 578 us; the launch traced here: 575 us
  waiting for transfers between devices  426 us (74%)
  local copies, waits for them, and re-layouts  66.9 us (12%)
  loops' own time  50.8 us (9%)
  matrix products  15.6 us (3%)
  between operations  13.4 us (2%)
    reduce_scatter x1, waiting for transfers between devices, body(): lax.psum_scatter(tile_products(tiles_all, left_block, right_block, is_liv...  373 us
    all_gather x1, waiting for transfers between devices, body(): gathered = lax.all_gather(panel_rows, 'row', axis=0, tiled=True)  53.2 us
    dynamic_update_slice x32, local copies, waits for them, and re-layouts, tile_products(): return lax.map(single, (lefts, rights, flags))  34.3 us
    dynamic_slice x46, local copies, waits for them, and re-layouts, tile_products(): return lax.map(single, (lefts, rights, flags))  29.7 us
    another operation x32, loops' own time, single(): return lax.cond(flag, compute, blank)  28.9 us
    another operation x1, loops' own time, tile_products(): return lax.map(single, (lefts, rights, flags))  21.9 us
    dot_general x7, matrix products, compute(): lax.dot_general(tiles_all[left_one], tiles_all[right_one], (((1,), (1,)),...  15.6 us
  transfers between devices with their start and end apart: 2, of which 2 were waited for; matrix products, arithmetic and copies ran while one was open for 0% of the time, Pallas kernels for 0%

commit v1 on v0

--- a/solution.py
+++ b/solution.py
@@ -4,6 +4,23 @@
 from jax.sharding import PartitionSpec as P
 
 BLOCK = 512
+
+
+def laid_out(blocks, dim):
+    blocks = jnp.moveaxis(blocks, 0, dim)
+    shape = blocks.shape
+    return blocks.reshape(*shape[:dim], shape[dim] * shape[dim + 1], *shape[dim + 2 :])
+
+
+def collected_by_bits(x, axis):
+    size, here = (lax.axis_size(axis), lax.axis_index(axis))
+    blocks, distance = (x[None], 1)
+    while distance < size:
+        theirs = lax.ppermute(blocks, axis, [(i, i ^ distance) for i in range(size)])
+        low = here & distance == 0
+        blocks = jnp.concatenate([jnp.where(low, blocks, theirs), jnp.where(low, theirs, blocks)])
+        distance *= 2
+    return blocks
 
 
 def slot_table(owner_slot, group_id, positions, per_group):
@@ -50,7 +67,7 @@
     row_tiles = per_group * (blocks - per_group) + per_group * (per_group + 1) // 2
     slot_count = (row_tiles + cols_n - 1) // cols_n
     positions = cols_n * slot_count
-    gathered = lax.all_gather(panel_rows, "row", axis=0, tiled=True)
+    gathered = laid_out(collected_by_bits(panel_rows, "row"), 0)
     my_group = lax.axis_index("row")
     left_block, right_block, is_live = slot_table(owner_slot, my_group, positions, per_group)
     tiles_all = gathered.reshape(blocks, BLOCK, inner_cols)

time: 578 us -> 673 us (1.16)
  waiting for transfers between devices: 426 us -> 507 us
  other arithmetic: 1.78 us -> 14.5 us
    ppermute x0 -> x3, waiting for transfers between devices: none -> 138 us  [collected_by_bits(): lax.ppermute(blocks, axis, [(i, i ^ distance) for i in range(size)])]
    all_gather x1 -> x0, waiting for transfers between devices: 53.2 us -> none  [body(): gathered = lax.all_gather(panel_rows, 'row', axis=0, tiled=True)]
    select_n x0 -> x3, other arithmetic: none -> 7.35 us  [collected_by_bits(): jnp.where(low, blocks, theirs)]
    concatenate x0 -> x3, other arithmetic: none -> 6.81 us  [collected_by_bits(): jnp.concatenate([jnp.where(low, blocks, theirs), jnp.where(low, theirs, b...]
  transfers between devices with their start and end apart: 2 -> 4, of which waited for: 2 -> 4; matrix products, arithmetic and copies ran while one was open for 0% -> 0% of each run, Pallas kernels for 0% -> 0%
where the time goes in v1:
time: 673 us; the launch traced here: 670 us
  waiting for transfers between devices  507 us (75%)
  local copies, waits for them, and re-layouts  65 us (10%)
  loops' own time  49 us (7%)
  matrix products  15.6 us (2%)
  other arithmetic  14.5 us (2%)
  between operations  13.4 us (2%)
    reduce_scatter x1, waiting for transfers between devices, body(): lax.psum_scatter(tile_products(tiles_all, left_block, right_block, is_liv...  369 us
    ppermute x3, waiting for transfers between devices, collected_by_bits(): lax.ppermute(blocks, axis, [(i, i ^ distance) for i in range(size)])  138 us
    dynamic_update_slice x32, local copies, waits for them, and re-layouts, tile_products(): return lax.map(single, (lefts, rights, flags))  34.1 us
    another operation x32, loops' own time, single(): return lax.cond(flag, compute, blank)  27.9 us
    dynamic_slice x46, local copies, waits for them, and re-layouts, tile_products(): return lax.map(single, (lefts, rights, flags))  26.9 us
    another operation x1, loops' own time, tile_products(): return lax.map(single, (lefts, rights, flags))  21.1 us
    dot_general x7, matrix products, compute(): lax.dot_general(tiles_all[left_one], tiles_all[right_one], (((1,), (1,)),...  15.6 us
  transfers between devices with their start and end apart: 4, of which 4 were waited for; matrix products, arithmetic and copies ran while one was open for 0% of the time, Pallas kernels for 0%

profile of v1, /device:TPU:1, one launch (start us, length us, event | category | flops | bytes accessed | tf_op | source)
XLA Modules:
  0.0 670.0 jit_solution(18443351076921023848)
XLA Ops:
  6.5 1.4 collective-permute-start
  7.9 2.5 collective-permute-done
  10.4 1.4 broadcast_select_fusion.5
  11.8 1.0 copy-done.1
  12.9 1.4 collective-permute-start.1
  14.3 45.6 %collective-permute-done.1 = f32[2,1024,256]{2,1,0:T(8,128)} collective-permute-done((f32[2,1024,256]{2,1,0:T(8,128)S(1)}, f32[2,1024,256]{2,1,0:T(8,128)}, u32[]{:S(2)}, u32[]{:S(2)}) %collective-permute-start.1) | collective-permute-done | bytes 2097184 | tf_op jit(solution)/shard_map/ppermute | solution.py:19
  59.9 2.1 broadcast_select_fusion.3
  62.1 2.5 pad_maximum_fusion.1
  64.7 2.9 collective-permute-start.2
  68.0 89.5 %collective-permute-done.2 = f32[4,1024,256]{2,1,0:T(8,128)} collective-permute-done((f32[4,1024,256]{2,1,0:T(8,128)}, f32[4,1024,256]{2,1,0:T(8,128)}, u32[]{:S(2)}, u32[]{:S(2)}) %collective-permute-start.2) | collective-permute-done | bytes 4194336 | tf_op jit(solution)/shard_map/ppermute | solution.py:19
  157.5 3.9 broadcast_select_fusion.1
  161.3 4.1 pad_maximum_fusion
  165.5 128.5 %while.10 = (s32[]{:T(128)}, f32[32,512,512]{2,1,0:T(8,128)}, pred[32]{0:T(512)(128)(4,1)S(1)}, s32[32]{0:T(128)S(1)}, f32[16,512,256]{2,1,0:T(8,128)}, /*index=5*/s32[32]{0:T(128)S(1)}, s32[]{:T(128)}) while((s32[]{:T(128)}, f32[32,512,512]{2,1,0:T(8,128)}, pred[32]{0:T(512)(128)(4,1)S(1)}, s32[32]{0:T(128)S(1)}, f32[16,512,256]{2,1,0:T(8,128)}, ...), condition=%wide.region_6.7_spmd, body=%wide.region_3.6_spmd.sunk | while | flops 805306368 | bytes 4195044 | solution.py:58
  166.7 7.3 %conditional.2 = (f32[1,512,512]{2,1,0:T(8,128)S(1)}) conditional(s32[]{:T(128)} %bitcast.17, () %tuple.34, (s32[32]{0:T(128)S(1)}, s32[]{:T(128)}, f32[16,512,256]{2,1,0:T(8,128)}, s32[32]{0:T(128)S(1)}) %tuple.35), branch_computations={%region_4.4_spmd, %region_5.5_spmd} | conditional | flops 805306368 | bytes 2097260 | solution.py:56
  171.8 2.2 convolution_bitcast_fusion
  174.0 1.0 constant_dynamic-update-slice_fusion.2
  176.4 1.1 constant_dynamic-update-slice_fusion.2
  178.9 1.1 constant_dynamic-update-slice_fusion.2
  181.4 1.1 constant_dynamic-update-slice_fusion.2
  183.8 1.1 constant_dynamic-update-slice_fusion.2
  186.2 1.1 constant_dynamic-update-slice_fusion.2
  188.5 7.3 %conditional.2 = (f32[1,512,512]{2,1,0:T(8,128)S(1)}) conditional(s32[]{:T(128)} %bitcast.17, () %tuple.34, (s32[32]{0:T(128)S(1)}, s32[]{:T(128)}, f32[16,512,256]{2,1,0:T(8,128)}, s32[32]{0:T(128)S(1)}) %tuple.35), branch_computations={%region_4.4_spmd, %region_5.5_spmd} | conditional | flops 805306368 | bytes 2097260 | solution.py:56
  188.6 0.6 dynamic_slice.18
  191.1 0.6 dynamic_slice.20
  193.6 2.2 convolution_bitcast_fusion
  195.9 1.1 constant_dynamic-update-slice_fusion.2
  198.3 1.1 constant_dynamic-update-slice_fusion.2
  200.6 7.3 %conditional.2 = (f32[1,512,512]{2,1,0:T(8,128)S(1)}) conditional(s32[]{:T(128)} %bitcast.17, () %tuple.34, (s32[32]{0:T(128)S(1)}, s32[]{:T(128)}, f32[16,512,256]{2,1,0:T(8,128)}, s32[32]{0:T(128)S(1)}) %tuple.35), branch_computations={%region_4.4_spmd, %region_5.5_spmd} | conditional | flops 805306368 | bytes 2097260 | solution.py:56
  200.6 0.6 dynamic_slice.18
  205.7 2.2 convolution_bitcast_fusion
  208.0 1.1 constant_dynamic-update-slice_fusion.2
  210.4 1.0 constant_dynamic-update-slice_fusion.2
  212.9 1.1 constant_dynamic-update-slice_fusion.2
  215.3 1.1 constant_dynamic-update-slice_fusion.2
  217.7 1.1 constant_dynamic-update-slice_fusion.2
  220.2 1.0 constant_dynamic-update-slice_fusion.2
  222.6 1.1 constant_dynamic-update-slice_fusion.2
  225.1 1.1 constant_dynamic-update-slice_fusion.2
  227.5 1.0 constant_dynamic-update-slice_fusion.2
  229.9 1.1 constant_dynamic-update-slice_fusion.2
  232.4 1.1 constant_dynamic-update-slice_fusion.2
  234.8 1.1 constant_dynamic-update-slice_fusion.2
  237.1 7.3 %conditional.2 = (f32[1,512,512]{2,1,0:T(8,128)S(1)}) conditional(s32[]{:T(128)} %bitcast.17, () %tuple.34, (s32[32]{0:T(128)S(1)}, s32[]{:T(128)}, f32[16,512,256]{2,1,0:T(8,128)}, s32[32]{0:T(128)S(1)}) %tuple.35), branch_computations={%region_4.4_spmd, %region_5.5_spmd} | conditional | flops 805306368 | bytes 2097260 | solution.py:56
  237.2 0.6 dynamic_slice.18
  242.2 2.2 convolution_bitcast_fusion
  244.5 1.1 constant_dynamic-update-slice_fusion.2
  246.8 7.3 %conditional.2 = (f32[1,512,512]{2,1,0:T(8,128)S(1)}) conditional(s32[]{:T(128)} %bitcast.17, () %tuple.34, (s32[32]{0:T(128)S(1)}, s32[]{:T(128)}, f32[16,512,256]{2,1,0:T(8,128)}, s32[32]{0:T(128)S(1)}) %tuple.35), branch_computations={%region_4.4_spmd, %region_5.5_spmd} | conditional | flops 805306368 | bytes 2097260 | solution.py:56
  251.8 2.2 convolution_bitcast_fusion
  254.1 1.1 constant_dynamic-update-slice_fusion.2
  256.5 1.1 constant_dynamic-update-slice_fusion.2
  258.8 7.3 %conditional.2 = (f32[1,512,512]{2,1,0:T(8,128)S(1)}) conditional(s32[]{:T(128)} %bitcast.17, () %tuple.34, (s32[32]{0:T(128)S(1)}, s32[]{:T(128)}, f32[16,512,256]{2,1,0:T(8,128)}, s32[32]{0:T(128)S(1)}) %tuple.35), branch_computations={%region_4.4_spmd, %region_5.5_spmd} | conditional | flops 805306368 | bytes 2097260 | solution.py:56
  263.9 2.2 convolution_bitcast_fusion
  266.2 1.1 constant_dynamic-update-slice_fusion.2
  268.6 1.1 constant_dynamic-update-slice_fusion.2
  271.1 1.0 constant_dynamic-update-slice_fusion.2
  273.5 1.1 constant_dynamic-update-slice_fusion.2
  275.9 1.1 constant_dynamic-update-slice_fusion.2
  278.4 1.1 constant_dynamic-update-slice_fusion.2
  280.9 1.0 constant_dynamic-update-slice_fusion.2
  283.3 1.1 constant_dynamic-update-slice_fusion.2
  285.6 7.3 %conditional.2 = (f32[1,512,512]{2,1,0:T(8,128)S(1)}) conditional(s32[]{:T(128)} %bitcast.17, () %tuple.34, (s32[32]{0:T(128)S(1)}, s32[]{:T(128)}, f32[16,512,256]{2,1,0:T(8,128)}, s32[32]{0:T(128)S(1)}) %tuple.35), branch_computations={%region_4.4_spmd, %region_5.5_spmd} | conditional | flops 805306368 | bytes 2097260 | solution.py:56
  290.7 2.2 convolution_bitcast_fusion
  292.9 1.1 constant_dynamic-update-slice_fusion.2
  294.0 369.2 %reduce-scatter.2.cloned.1.call-done = f32[2,512,512]{2,1,0:T(8,128)} async-done(((f32[32,512,512]{2,1,0:T(8,128)}), f32[2,512,512]{2,1,0:T(8,128)}) %reduce-scatter.2.cloned.1.call-update) | async-done | bytes 2097168 | tf_op jit(solution)/shard_map/reduce_scatter | solution.py:74
  (105 shorter events, 31.6 us)
Async XLA Ops:
  6.5 656.7 %reduce-scatter.2.cloned.1.call-start = ((), (), s32[]{:S(2)}) async-start(), calls=%async_computation.1 | async-start | bytes 35651584 | tf_op jit(solution)/shard_map/reduce_scatter | solution.py:74
  6.5 3.9 collective-permute-start
  11.8 1.0 copy-start.1
  12.9 47.0 %collective-permute-start.1 = (f32[2,1024,256]{2,1,0:T(8,128)S(1)}, f32[2,1024,256]{2,1,0:T(8,128)}, u32[]{:S(2)}, u32[]{:S(2)}) collective-permute-start(f32[2,1024,256]{2,1,0:T(8,128)S(1)} %pad_maximum_fusion.2), channel_id=1, source_target_pairs={{0,32},{16,48},{32,0},{48,16},{64,96},{80,112},{96,64},{112,80},{1... | collective-permute-start | bytes 6291464 | tf_op jit(solution)/shard_map/ppermute | solution.py:19
  62.0 2.7 copy-start
  62.0 5.6 copy-start.2
  64.7 92.7 %collective-permute-start.2 = (f32[4,1024,256]{2,1,0:T(8,128)}, f32[4,1024,256]{2,1,0:T(8,128)}, u32[]{:S(2)}, u32[]{:S(2)}) collective-permute-start(f32[4,1024,256]{2,1,0:T(8,128)} %pad_maximum_fusion.1), channel_id=1, source_target_pairs={{0,64},{16,80},{32,96},{48,112},{64,0},{80,16},{96,32},{112,48},{1... | collective-permute-start | bytes 12582920 | tf_op jit(solution)/shard_map/ppermute | solution.py:19
Sparse Core Ops, SparseCore 0:
  294.1 369.0 reduce-scatter.1
